TPU v7x, 32 devices: a whole 2x2x4 slice. The times are simulated.
32 devices in a mesh: grp: 4 (over x, core), mem: 8 (over z, y).
Axes of the slice: x: 2, y: 2, z: 4, core: 2. Of those that a mesh axis runs over, the one named last changes fastest.
Arguments:
- source_pts: float32 [64, 8192], P(None, ('grp', 'mem')), may hold values from -30 to 30
- target_pts: float32 [64, 8192], P(None, ('grp', 'mem')), may hold values from -30 to 30
- source_pot: float32 [8192], P(('grp', 'mem')), may hold values from -8 to 520
- target_pot: float32 [8192], P(('grp', 'mem')), may hold values from -8 to 520
- source_logw: float32 [8192], P(('grp', 'mem')), may hold values from -1 to 4
- target_logw: float32 [8192], P(('grp', 'mem')), may hold values from -1 to 4
Outputs:
- source_new: float32 [8192], P(('grp', 'mem'))
- target_new: float32 [8192], P(('grp', 'mem'))
All inputs are finite; a program needn't handle non-finite values.
Results may differ from a plain program's by a relative error of at most 0.0001.
Values sent between devices are 32-bit elements; how exact they have to be, the bound alone decides.
A program may use at most 64 MiB of HBM per device.

v0:
```python
import math
import jax
import jax.numpy as jnp
from jax import lax
from jax.sharding import PartitionSpec as P

epsilon = 4.0
floor_value = -1e30


def sweep(carry, points, squares, row_term, moving, offset):
    count = moving.shape[1]
    limit = 128
    width = math.gcd(count, limit)

    def block(index, state):
        row_max, row_sum, col_max, col_sum = state
        begin = index * width
        cols = lax.dynamic_slice_in_dim(moving, begin, width, 1)
        ycols = cols[:-1]
        cvals = cols[-1]
        ysq = 0.5 * jnp.sum(ycols * ycols, 0)
        cross = lax.dot_general(
            points,
            ycols,
            (((0,), (0,)), ((), ())),
            precision=lax.Precision.HIGHEST,
            preferred_element_type=jnp.float32,
        )
        half = (squares[:, None] + ysq[None, :] - cross) / epsilon
        scores = cvals[None, :] - half
        new_row = jnp.maximum(row_max, jnp.max(scores, 1))
        row_sum = row_sum * jnp.exp(row_max - new_row) + jnp.sum(
            jnp.exp(scores - new_row[:, None]), 1
        )
        others = row_term[:, None] - half
        place = offset + begin
        old_max = lax.dynamic_slice_in_dim(col_max, place, width, 0)
        old_sum = lax.dynamic_slice_in_dim(col_sum, place, width, 0)
        new_col = jnp.maximum(old_max, jnp.max(others, 0))
        new_sum = old_sum * jnp.exp(old_max - new_col) + jnp.sum(
            jnp.exp(others - new_col[None, :]), 0
        )
        col_max = lax.dynamic_update_slice_in_dim(col_max, new_col, place, 0)
        col_sum = lax.dynamic_update_slice_in_dim(col_sum, new_sum, place, 0)
        return (new_row, row_sum, col_max, col_sum)

    return lax.fori_loop(0, count // width, block, carry)


def totals(source_logw, target_logw):
    peaks = lax.pmax((jnp.max(source_logw), jnp.max(target_logw)), ("grp", "mem"))
    masses = lax.psum(
        (jnp.sum(jnp.exp(source_logw - peaks[0])), jnp.sum(jnp.exp(target_logw - peaks[1]))),
        ("grp", "mem"),
    )
    return (peaks[0] + jnp.log(masses[0]), peaks[1] + jnp.log(masses[1]))


def local(source_pts, target_pts, source_pot, target_pot, source_logw, target_logw):
    members = lax.axis_size("mem")
    rows = source_pts.shape[1]
    outer = rows * members
    src_norm, tgt_norm = totals(source_logw, target_logw)
    row_term = source_logw - src_norm + source_pot / epsilon
    col_term = target_logw - tgt_norm + target_pot / epsilon
    moving = jnp.concatenate([target_pts, col_term[None, :]], 0)
    standing = jnp.concatenate([source_pts, row_term[None, :]], 0)
    row_block = lax.all_gather(standing, "mem", axis=1, tiled=True)
    col_block = lax.all_gather(moving, "grp", axis=1, tiled=True)
    block_pts = row_block[:-1]
    block_terms = row_block[-1]
    block_sq = 0.5 * jnp.sum(block_pts * block_pts, 0)
    span = col_block.shape[1]
    carry = (
        jnp.full((outer,), floor_value, jnp.float32),
        jnp.zeros((outer,), jnp.float32),
        jnp.full((span,), floor_value, jnp.float32),
        jnp.zeros((span,), jnp.float32),
    )
    row_max, row_sum, col_max, col_sum = sweep(
        carry, block_pts, block_sq, block_terms, col_block, 0
    )
    rpeak = lax.pmax(row_max, "mem")
    own_rsum = lax.psum_scatter(
        row_sum * jnp.exp(row_max - rpeak), "mem", scatter_dimension=0, tiled=True
    )
    own_rmax = lax.dynamic_slice_in_dim(rpeak, lax.axis_index("mem") * rows, rows, 0)
    row_total = own_rmax + jnp.log(own_rsum)
    cpeak = lax.pmax(col_max, "grp")
    own_sum = lax.psum_scatter(
        col_sum * jnp.exp(col_max - cpeak), "grp", scatter_dimension=0, tiled=True
    )
    own_max = lax.dynamic_slice_in_dim(cpeak, lax.axis_index("grp") * rows, rows, 0)
    col_total = own_max + jnp.log(own_sum)
    row_hat = -epsilon * row_total
    col_hat = -epsilon * col_total
    return (0.5 * (source_pot + row_hat), 0.5 * (target_pot + col_hat))


def solution(mesh):
    return jax.shard_map(
        local,
        mesh=mesh,
        in_specs=(
            P(None, ("grp", "mem")),
            P(None, ("grp", "mem")),
            P(("grp", "mem")),
            P(("grp", "mem")),
            P(("grp", "mem")),
            P(("grp", "mem")),
        ),
        out_specs=(P(("grp", "mem")), P(("grp", "mem"))),
        check_vma=False,
    )
```

profile of v0, /device:TPU:0, one launch (start us, length us, event | category | flops | bytes accessed | tf_op | source)
XLA Modules:
  0.0 205.6 jit_solution(15678545301726195394)
XLA Ops:
  0.6 0.0 copy-start.2
  0.6 1.3 reduce_max.44
  1.9 0.0 copy-done.2
  1.9 0.6 reduce_max.45
  2.5 42.2 %all-reduce.3 = (f32[]{:T(128)}, f32[]{:T(128)}) all-reduce(f32[]{:T(128)} %reduce_max.44, f32[]{:T(128)} %reduce_max.45), channel_id=1, replica_groups=mesh['grp'=4,'mem'=8] {'grp','mem'}, use_global_device_ids=true, to_apply=%region_1.0 | all-reduce | flops 2 | bytes 16 | tf_op jit(solution)/shard_map/pmax | solution.py:52
  44.8 0.7 copy-done.3
  45.4 2.0 exponential_reduce_fusion.2
  47.4 40.6 %all-reduce.2 = (f32[]{:T(128)}, f32[]{:T(128)}) all-reduce(f32[]{:T(128)} %get-tuple-element.225, f32[]{:T(128)} %get-tuple-element.224), channel_id=1, replica_groups=mesh['grp'=4,'mem'=8] {'grp','mem'}, use_global_device_ids=true, to_apply=%region_3.0 | all-reduce | flops 2 | bytes 16 | tf_op jit(solution)/shard_map/psum | solution.py:53
  88.6 0.0 copy-start.5
  89.3 0.0 copy-done.5
  89.3 0.8 pad_maximum_fusion.1
  90.2 31.4 %all_gather.7 = f32[65,2048]{1,0:T(8,128)S(1)} all-gather(f32[65,256]{1,0:T(8,128)S(1)} %pad_maximum_fusion.1), channel_id=1, replica_groups=mesh['grp'=4,'mem'=8] {'mem'}, dimensions={1}, use_global_device_ids=true | all-gather | bytes 599040 | tf_op jit(solution)/shard_map/all_gather | solution.py:69
  121.6 0.0 copy-start
  121.6 0.1 fusion.14
  121.7 0.7 copy-done
  123.0 0.0 copy-start.4
  123.7 0.0 copy-done.4
  123.7 0.0 copy-done.1
  123.8 6.7 %all_gather.6 = f32[65,1024]{1,0:T(8,128)S(1)} all-gather(f32[65,256]{1,0:T(8,128)S(1)} %pad_maximum_fusion), channel_id=1, replica_groups=mesh['grp'=4,'mem'=8] {'grp'}, dimensions={1}, use_global_device_ids=true | all-gather | bytes 332800 | tf_op jit(solution)/shard_map/all_gather | solution.py:70
  130.5 0.7 slice-done
  131.2 18.0 %while.20 = (s32[]{:T(128)}, f32[2048]{0:T(1024)S(1)}, f32[2048]{0:T(1024)S(1)}, f32[1024]{0:T(1024)S(1)}, f32[1024]{0:T(1024)S(1)}, /*index=5*/f32[65,1024]{1,0...) while((s32[]{:T(128)}, f32[2048]{0:T(1024)S(1)}, ...), condition=%wide.region_15.0_spmd.clone, body=%wide.region_9.0_spmd.clone.sunk | while | flops 204761344 | bytes 2844898 | solution.py:48
  131.2 1.3 subtract_reduce_fusion.3
  132.6 0.2 fusion.20
  132.7 0.4 exponential_reduce_fusion.5
  133.2 0.2 add_dynamic-update-slice_fusion.2
  133.5 1.3 subtract_reduce_fusion.3
  134.8 0.2 fusion.20
  135.0 0.4 exponential_reduce_fusion.5
  135.4 0.2 add_dynamic-update-slice_fusion.2
  135.7 1.3 subtract_reduce_fusion.3
  137.1 0.2 fusion.20
  137.3 0.4 exponential_reduce_fusion.5
  137.7 0.2 add_dynamic-update-slice_fusion.2
  138.0 1.3 subtract_reduce_fusion.3
  139.3 0.2 fusion.20
  139.5 0.4 exponential_reduce_fusion.5
  139.9 0.2 add_dynamic-update-slice_fusion.2
  140.2 1.3 subtract_reduce_fusion.3
  141.6 0.2 fusion.20
  141.8 0.4 exponential_reduce_fusion.5
  142.2 0.2 add_dynamic-update-slice_fusion.2
  142.5 1.3 subtract_reduce_fusion.3
  143.8 0.2 fusion.20
  144.0 0.4 exponential_reduce_fusion.5
  144.5 0.2 add_dynamic-update-slice_fusion.2
  144.8 1.3 subtract_reduce_fusion.3
  146.1 0.2 fusion.20
  146.3 0.4 exponential_reduce_fusion.5
  146.7 0.2 add_dynamic-update-slice_fusion.2
  147.0 1.3 subtract_reduce_fusion.3
  148.3 0.2 fusion.20
  148.5 0.4 exponential_reduce_fusion.5
  149.0 0.2 add_dynamic-update-slice_fusion.2
  149.2 7.1 %pmax.31 = f32[1024]{0:T(1024)S(1)} all-reduce(f32[1024]{0:T(1024)S(1)} %get-tuple-element.161), channel_id=1, replica_groups=mesh['grp'=4,'mem'=8] {'grp'}, use_global_device_ids=true, to_apply=%region_18.0 | all-reduce | flops 1024 | bytes 8192 | tf_op jit(solution)/shard_map/pmax | solution.py:90
  156.3 6.0 %all-reduce.1 = f32[1024]{0:T(1024)S(1)} all-reduce(f32[1024]{0:T(1024)S(1)} %exponential_multiply_fusion.1), channel_id=3, replica_groups=mesh['grp'=4,'mem'=8] {'grp'}, use_global_device_ids=true, to_apply=%region_19.0.clone | all-reduce | flops 1024 | bytes 8192
  162.3 0.6 copy-done.7
  162.9 0.6 dynamic-slice.2
  164.2 0.7 fusion.12
  164.8 20.8 %pmax.30 = f32[2048]{0:T(1024)S(1)} all-reduce(f32[2048]{0:T(1024)S(1)} %get-tuple-element.159), channel_id=1, replica_groups=mesh['grp'=4,'mem'=8] {'mem'}, use_global_device_ids=true, to_apply=%region_16.0 | all-reduce | flops 2048 | bytes 16384 | tf_op jit(solution)/shard_map/pmax | solution.py:84
  185.7 17.4 %all-reduce = f32[2048]{0:T(1024)S(1)} all-reduce(f32[2048]{0:T(1024)S(1)} %exponential_multiply_fusion), channel_id=2, replica_groups=mesh['grp'=4,'mem'=8] {'mem'}, use_global_device_ids=true, to_apply=%region_17.0.clone | all-reduce | flops 2048 | bytes 16384
  203.1 0.0 copy-start.6
  203.1 0.6 copy-done.6
  203.7 0.6 dynamic-slice
  205.0 0.7 fusion.11
  (78 shorter events, 0.6 us)
Async XLA Ops:
  0.6 1.3 copy-start.2
  44.8 0.7 copy-start.3
  88.6 0.7 copy-start.5
  121.6 0.8 copy-start
  121.6 2.1 %copy-start.1 = (f32[64,256]{1,0:T(8,128)S(1)}, f32[64,256]{1,0:T(8,128)}, u32[]{:S(2)}) copy-start(f32[64,256]{1,0:T(8,128)} %param.9) | copy-start | bytes 196612
  123.0 0.7 copy-start.4
  130.5 0.7 slice-start
  162.3 0.7 copy-start.7
  203.1 0.7 copy-start.6
where the time goes:
time: 206 us
  blocking collectives  172 us (83%)
  other arithmetic  13 us (6%)
  matrix products  10.4 us (5%)
  local copies, waits for them, and re-layouts  4.74 us (2%)
  between operations  4.67 us (2%)
    pmax x1, blocking collectives, totals(): lax.pmax((jnp.max(source_logw), jnp.max(target_logw)), ('grp', 'mem'))  42.2 us
    psum x1, blocking collectives, totals(): lax.psum((jnp.sum(jnp.exp(source_logw - peaks[0])), jnp.sum(jnp.exp(targe...  40.6 us
    all_gather x1, blocking collectives, local(): row_block = lax.all_gather(standing, 'mem', axis=1, tiled=True)  31.4 us
    unnamed x2, blocking collectives  23.4 us
    pmax x1, blocking collectives, local(): rpeak = lax.pmax(row_max, 'mem')  20.8 us
    dot_general x8, matrix products, block(): lax.dot_general(points, ycols, (((0,), (0,)), ((), ())), precision=lax.Pr...  10.4 us
    pmax x1, blocking collectives, local(): cpeak = lax.pmax(col_max, 'grp')  7.05 us
    all_gather x1, blocking collectives, local(): col_block = lax.all_gather(moving, 'grp', axis=1, tiled=True)  6.72 us

commit v1 on v0

--- a/solution.py
+++ b/solution.py
@@ -51,8 +51,11 @@
 def totals(source_logw, target_logw):
     peaks = lax.pmax((jnp.max(source_logw), jnp.max(target_logw)), ("grp", "mem"))
     masses = lax.psum(
-        (jnp.sum(jnp.exp(source_logw - peaks[0])), jnp.sum(jnp.exp(target_logw - peaks[1]))),
-        ("grp", "mem"),
+        lax.psum(
+            (jnp.sum(jnp.exp(source_logw - peaks[0])), jnp.sum(jnp.exp(target_logw - peaks[1]))),
+            "grp",
+        ),
+        "mem",
     )
     return (peaks[0] + jnp.log(masses[0]), peaks[1] + jnp.log(masses[1]))
 

time: 206 us -> 191 us (0.927)
  blocking collectives: 172 us -> 157 us
    psum x1, blocking collectives: 40.6 us -> 6.51 us  [totals(): lax.psum((jnp.sum(jnp.exp(source_logw - peaks[0])), jnp.sum(jnp.exp(targe...]
    psum x0 -> x1, blocking collectives: none -> 22 us  [totals(): lax.psum(lax.psum((jnp.sum(jnp.exp(source_logw - peaks[0])), jnp.sum(jnp....]
    pmax x1, blocking collectives: 20.8 us -> 17.4 us  [local(): rpeak = lax.pmax(row_max, 'mem')]
where the time goes in v1:
time: 191 us; the launch traced here: 190 us
  blocking collectives  157 us (82%)
  other arithmetic  13 us (7%)
  matrix products  10.4 us (5%)
  local copies, waits for them, and re-layouts  4.74 us (2%)
  between operations  4.67 us (2%)
    pmax x1, blocking collectives, totals(): lax.pmax((jnp.max(source_logw), jnp.max(target_logw)), ('grp', 'mem'))  42.2 us
    all_gather x1, blocking collectives, local(): row_block = lax.all_gather(standing, 'mem', axis=1, tiled=True)  31.6 us
    unnamed x2, blocking collectives  25.1 us
    psum x1, blocking collectives, totals(): lax.psum(lax.psum((jnp.sum(jnp.exp(source_logw - peaks[0])), jnp.sum(jnp....  22 us
    pmax x1, blocking collectives, local(): rpeak = lax.pmax(row_max, 'mem')  17.4 us
    dot_general x8, matrix products, block(): lax.dot_general(points, ycols, (((0,), (0,)), ((), ())), precision=lax.Pr...  10.4 us
    psum x1, blocking collectives, totals(): lax.psum((jnp.sum(jnp.exp(source_logw - peaks[0])), jnp.sum(jnp.exp(targe...  6.51 us
    pmax x1, blocking collectives, local(): cpeak = lax.pmax(col_max, 'grp')  6.2 us

profile of v1, /device:TPU:0, one launch (start us, length us, event | category | flops | bytes accessed | tf_op | source)
XLA Modules:
  0.0 190.2 jit_solution(13796606693855869674)
XLA Ops:
  0.6 0.0 copy-start.2
  0.6 1.3 reduce_max.44
  1.9 0.0 copy-done.2
  1.9 0.6 reduce_max.45
  2.5 42.2 %all-reduce.2 = (f32[]{:T(128)}, f32[]{:T(128)}) all-reduce(f32[]{:T(128)} %reduce_max.44, f32[]{:T(128)} %reduce_max.45), channel_id=1, replica_groups=mesh['grp'=4,'mem'=8] {'grp','mem'}, use_global_device_ids=true, to_apply=%region_1.0 | all-reduce | flops 2 | bytes 16 | tf_op jit(solution)/shard_map/pmax | solution.py:52
  44.7 0.7 copy-done.3
  45.4 2.0 %exponential_reduce_fusion.2 = (f32[]{:T(128)}, f32[]{:T(128)}) fusion(f32[256]{0:T(256)S(1)} %copy-done.2, f32[]{:T(128)} %get-tuple-element.216, f32[256]{0:T(256)S(1)} %copy-done.3, f32[]{:T(128)} %get-tuple-element.215), kind=kLoop, calls=%fused_computation.32 | loop fusion | flops 1022 | bytes 2064 | tf_op jit(solution)/shard_map/reduce_sum | solution.py:55
  47.4 6.5 %all-reduce.4 = (f32[]{:T(128)}, f32[]{:T(128)}) all-reduce(f32[]{:T(128)} %get-tuple-element.227, f32[]{:T(128)} %get-tuple-element.226), channel_id=1, replica_groups=mesh['grp'=4,'mem'=8] {'grp'}, use_global_device_ids=true, to_apply=%region_3.0 | all-reduce | flops 2 | bytes 16 | tf_op jit(solution)/shard_map/psum | solution.py:54
  53.9 22.0 %all-reduce.3 = (f32[]{:T(128)}, f32[]{:T(128)}) all-reduce(f32[]{:T(128)} %get-tuple-element.219, f32[]{:T(128)} %get-tuple-element.220), channel_id=1, replica_groups=mesh['grp'=4,'mem'=8] {'mem'}, use_global_device_ids=true, to_apply=%region_4.0 | all-reduce | flops 2 | bytes 16 | tf_op jit(solution)/shard_map/psum | solution.py:53
  76.6 0.0 copy-start.5
  77.2 0.0 copy-done.5
  77.2 0.8 pad_maximum_fusion.1
  78.1 31.6 %all_gather.7 = f32[65,2048]{1,0:T(8,128)S(1)} all-gather(f32[65,256]{1,0:T(8,128)S(1)} %pad_maximum_fusion.1), channel_id=1, replica_groups=mesh['grp'=4,'mem'=8] {'mem'}, dimensions={1}, use_global_device_ids=true | all-gather | bytes 599040 | tf_op jit(solution)/shard_map/all_gather | solution.py:72
  109.7 0.1 fusion.14
  109.7 0.7 copy-done
  111.1 0.0 copy-start.4
  111.7 0.0 copy-done.4
  111.8 0.0 copy-done.1
  111.8 5.9 %all_gather.6 = f32[65,1024]{1,0:T(8,128)S(1)} all-gather(f32[65,256]{1,0:T(8,128)S(1)} %pad_maximum_fusion), channel_id=1, replica_groups=mesh['grp'=4,'mem'=8] {'grp'}, dimensions={1}, use_global_device_ids=true | all-gather | bytes 332800 | tf_op jit(solution)/shard_map/all_gather | solution.py:73
  117.7 0.7 slice-done
  118.3 18.0 %while.20 = (s32[]{:T(128)}, f32[2048]{0:T(1024)S(1)}, f32[2048]{0:T(1024)S(1)}, f32[1024]{0:T(1024)S(1)}, f32[1024]{0:T(1024)S(1)}, /*index=5*/f32[65,1024]{1,0...) while((s32[]{:T(128)}, f32[2048]{0:T(1024)S(1)}, ...), condition=%wide.region_17.0_spmd.clone, body=%wide.region_11.0_spmd.clone.sunk | while | flops 204761344 | bytes 2844898 | solution.py:48
  118.4 1.3 subtract_reduce_fusion.3
  119.7 0.2 fusion.20
  119.9 0.4 exponential_reduce_fusion.5
  120.3 0.2 add_dynamic-update-slice_fusion.2
  120.6 1.3 subtract_reduce_fusion.3
  122.0 0.2 fusion.20
  122.2 0.4 exponential_reduce_fusion.5
  122.6 0.2 add_dynamic-update-slice_fusion.2
  122.9 1.3 subtract_reduce_fusion.3
  124.2 0.2 fusion.20
  124.4 0.4 exponential_reduce_fusion.5
  124.8 0.2 add_dynamic-update-slice_fusion.2
  125.2 1.3 subtract_reduce_fusion.3
  126.5 0.2 fusion.20
  126.7 0.4 exponential_reduce_fusion.5
  127.1 0.2 add_dynamic-update-slice_fusion.2
  127.4 1.3 subtract_reduce_fusion.3
  128.7 0.2 fusion.20
  128.9 0.4 exponential_reduce_fusion.5
  129.4 0.2 add_dynamic-update-slice_fusion.2
  129.7 1.3 subtract_reduce_fusion.3
  131.0 0.2 fusion.20
  131.2 0.4 exponential_reduce_fusion.5
  131.6 0.2 add_dynamic-update-slice_fusion.2
  131.9 1.3 subtract_reduce_fusion.3
  133.3 0.2 fusion.20
  133.4 0.4 exponential_reduce_fusion.5
  133.9 0.2 add_dynamic-update-slice_fusion.2
  134.2 1.3 subtract_reduce_fusion.3
  135.5 0.2 fusion.20
  135.7 0.4 exponential_reduce_fusion.5
  136.1 0.2 add_dynamic-update-slice_fusion.2
  136.4 6.2 %pmax.31 = f32[1024]{0:T(1024)S(1)} all-reduce(f32[1024]{0:T(1024)S(1)} %get-tuple-element.161), channel_id=1, replica_groups=mesh['grp'=4,'mem'=8] {'grp'}, use_global_device_ids=true, to_apply=%region_20.0 | all-reduce | flops 1024 | bytes 8192 | tf_op jit(solution)/shard_map/pmax | solution.py:93
  142.6 5.7 %all-reduce.1 = f32[1024]{0:T(1024)S(1)} all-reduce(f32[1024]{0:T(1024)S(1)} %exponential_multiply_fusion.1), channel_id=3, replica_groups=mesh['grp'=4,'mem'=8] {'grp'}, use_global_device_ids=true, to_apply=%region_21.0.clone | all-reduce | flops 1024 | bytes 8192
  148.3 0.6 copy-done.7
  148.9 0.6 dynamic-slice.2
  150.1 0.7 fusion.12
  150.8 17.4 %pmax.30 = f32[2048]{0:T(1024)S(1)} all-reduce(f32[2048]{0:T(1024)S(1)} %get-tuple-element.159), channel_id=1, replica_groups=mesh['grp'=4,'mem'=8] {'mem'}, use_global_device_ids=true, to_apply=%region_18.0 | all-reduce | flops 2048 | bytes 16384 | tf_op jit(solution)/shard_map/pmax | solution.py:87
  168.2 19.4 %all-reduce = f32[2048]{0:T(1024)S(1)} all-reduce(f32[2048]{0:T(1024)S(1)} %exponential_multiply_fusion), channel_id=2, replica_groups=mesh['grp'=4,'mem'=8] {'mem'}, use_global_device_ids=true, to_apply=%region_19.0.clone | all-reduce | flops 2048 | bytes 16384
  187.6 0.0 copy-start.6
  187.6 0.6 copy-done.6
  188.3 0.6 dynamic-slice
  189.5 0.7 fusion.11
  (79 shorter events, 0.6 us)
Async XLA Ops:
  0.6 1.3 copy-start.2
  44.7 0.7 copy-start.3
  76.6 0.7 copy-start.5
  109.6 0.8 copy-start
  109.7 2.1 %copy-start.1 = (f32[64,256]{1,0:T(8,128)S(1)}, f32[64,256]{1,0:T(8,128)}, u32[]{:S(2)}) copy-start(f32[64,256]{1,0:T(8,128)} %param.9) | copy-start | bytes 196612
  111.1 0.7 copy-start.4
  117.7 0.7 slice-start
  148.2 0.7 copy-start.7
  187.6 0.7 copy-start.6
